TPU v7x, 32 devices: a whole 2x2x4 slice. The times are simulated.
32 devices in a mesh: node: 8 (over z, x), expert: 4 (over y, core).
Axes of the slice: x: 2, y: 2, z: 4, core: 2. Of those that a mesh axis runs over, the one named last changes fastest.
Arguments:
- tokens: bfloat16 [16384, 1024], P(('node', 'expert')), may hold values from -6 to 6
- queries: bfloat16 [16384, 1024], P(('node', 'expert')), may hold values from -6 to 6
- keys: bfloat16 [16384, 1024], P(('node', 'expert')), may hold values from -6 to 6
- values: bfloat16 [16384, 1024], P(('node', 'expert')), may hold values from -12 to 12
- neighbours: int32 [128, 8], P(('node', 'expert')), may hold values from 0 to 127, as said below
- live_bits: int32 [128, 8], P(('node', 'expert')), may hold values from 0 to 1, as said below
- out_proj: bfloat16 [1024, 1024], replicated, may hold values from -0.1875 to 0.1875
- norm_gain: float32 [1024], replicated, may hold values from 0.5 to 1.5
- router: bfloat16 [1024, 32], replicated, may hold values from -0.1875 to 0.1875
- expert: int32 [16384], P(('node', 'expert')), may hold values from 0 to 31, as said below
- slot: int32 [16384], P(('node', 'expert')), may hold values from 0 to 31, as said below
- w_up: bfloat16 [32, 1024, 4096], P(('node', 'expert')), may hold values from -0.1875 to 0.1875
- w_down: bfloat16 [32, 4096, 1024], P(('node', 'expert')), may hold values from -0.09375 to 0.09375
Outputs:
- layer_out: bfloat16 [16384, 1024], P(('node', 'expert'))
Inputs may be any that keep to these rules, and one draw needn't show every extreme that they name: Tile g is held by device g // 4 in node-major order. neighbours[g, 0] is g itself; every listed tile is held by g's device or by the device one step before or after it along node with the same expert index (wrapping around); entry 1 is always one step before and entry 2 one step after. `live_bits`: entry 0 of every row is 1. Within the 512 tokens of one device, no two tokens share both expert and slot; some expert takes all 32 slots of every device. See expert: pairs (expert, slot) are distinct within one device's tokens.
All inputs are finite; a program needn't handle non-finite values.
Results may differ from a plain program's by a relative error of at most 0.0049.
Values may be sent and summed in bfloat16 or wider, within the bound.
A program may use at most 192 MiB of HBM per device.

v0:
```python
import jax
import jax.numpy as jnp
from jax import lax
from jax.sharding import PartitionSpec as P

D = 1024
HEADS = 16
HEAD_DIM = 64
TILE = 128
NB = 8
score_scale = 0.125


def extended(shard, sides, width):
    for axis, dim in sides:
        size, length = (lax.axis_size(axis), shard.shape[dim])
        up = [(i, (i + 1) % size) for i in range(size)]
        down = [(j, i) for i, j in up]
        last = lax.slice_in_dim(shard, length - width, length, axis=dim)
        leading = lax.slice_in_dim(shard, 0, width, axis=dim)
        before = lax.ppermute(last, axis, up)
        after = lax.ppermute(leading, axis, down)
        shard = jnp.concatenate([before, shard, after], axis=dim)
    return shard


def shards(
    tokens,
    queries,
    keys,
    values,
    neighbours,
    live_bits,
    out_proj,
    norm_gain,
    router,
    expert,
    slot,
    w_up,
    w_down,
):
    tok_dev = tokens.shape[0]
    tiles_dev = tok_dev // TILE
    experts = router.shape[1]
    cap = 2 * tok_dev // experts
    both = jnp.concatenate([keys, values], axis=1)
    widened = extended(both, (("node", 0),), tok_dev)
    window_tiles = widened.reshape(3 * tiles_dev, TILE, 2 * D)
    my_node = lax.axis_index("node")
    node_count = lax.axis_size("node")
    column_count = lax.axis_size("expert")
    owner_node = neighbours // tiles_dev // column_count
    offset = (owner_node - my_node + node_count) % node_count
    block_of = jnp.where(offset == 0, 1, jnp.where(offset == 1, 2, 0))
    position = block_of * tiles_dev + neighbours % tiles_dev
    gathered = window_tiles[position]
    near_keys = gathered[..., :D].reshape(tiles_dev, NB * TILE, HEADS, HEAD_DIM)
    near_values = gathered[..., D:].reshape(tiles_dev, NB * TILE, HEADS, HEAD_DIM)
    query_tiles = queries.reshape(tiles_dev, TILE, HEADS, HEAD_DIM)
    scores = (
        jnp.einsum("tqhd,tkhd->thqk", query_tiles, near_keys, preferred_element_type=jnp.float32)
        * score_scale
    )
    visible = jnp.repeat(live_bits, TILE, axis=1) > 0
    masked = jnp.where(visible[:, None, None, :], scores, -jnp.inf)
    peak = jnp.max(masked, axis=-1, keepdims=True)
    weights = jnp.exp(masked - peak)
    weights = (weights / jnp.sum(weights, axis=-1, keepdims=True)).astype(jnp.bfloat16)
    mixed = jnp.einsum("thqk,tkhd->tqhd", weights, near_values, preferred_element_type=jnp.float32)
    attn = mixed.reshape(tok_dev, D).astype(jnp.bfloat16)
    hidden = tokens.astype(jnp.float32) + jnp.dot(
        attn, out_proj, preferred_element_type=jnp.float32
    )
    spread = jnp.mean(hidden * hidden, axis=-1, keepdims=True)
    normed = (hidden * lax.rsqrt(spread + 1e-06) * norm_gain[None, :]).astype(jnp.bfloat16)
    logits = jnp.dot(normed, router, preferred_element_type=jnp.float32)
    columns = lax.iota(jnp.int32, experts)
    chosen = jnp.sum(jnp.where(columns[None, :] == expert[:, None], logits, 0.0), axis=-1)
    gate = jax.nn.sigmoid(chosen)
    slot_cell = expert * cap + slot
    one_hot = (lax.iota(jnp.int32, experts * cap)[:, None] == slot_cell[None, :]).astype(
        jnp.bfloat16
    )
    outgoing = jnp.dot(one_hot, normed, preferred_element_type=jnp.float32).astype(jnp.bfloat16)
    up_matrix = w_up[0]
    down_matrix = w_down[0]
    block = lax.all_to_all(
        outgoing.reshape(experts, 1, cap, D),
        ("node", "expert"),
        split_axis=0,
        concat_axis=1,
        tiled=True,
    )
    token_rows = block.reshape(-1, D)
    lifted = jnp.dot(token_rows, up_matrix, preferred_element_type=jnp.float32)
    lifted = jax.nn.gelu(lifted, approximate=True).astype(jnp.bfloat16)
    result = jnp.dot(lifted, down_matrix, preferred_element_type=jnp.float32).astype(jnp.bfloat16)
    returned = lax.all_to_all(
        result.reshape(block.shape), ("node", "expert"), split_axis=1, concat_axis=0, tiled=True
    )
    flat_back = returned.reshape(experts * cap, D)
    expert_out = jnp.einsum("ct,cd->td", one_hot, flat_back, preferred_element_type=jnp.float32)
    layer_out = hidden + gate[:, None] * expert_out
    return layer_out.astype(jnp.bfloat16)


def solution(mesh):
    in_specs = (
        P(("node", "expert"), None),
        P(("node", "expert"), None),
        P(("node", "expert"), None),
        P(("node", "expert"), None),
        P(("node", "expert"), None),
        P(("node", "expert"), None),
        P(),
        P(),
        P(),
        P(("node", "expert")),
        P(("node", "expert")),
        P(("node", "expert"), None, None),
        P(("node", "expert"), None, None),
    )
    out_specs = P(("node", "expert"), None)
    return jax.shard_map(shards, mesh=mesh, in_specs=in_specs, out_specs=out_specs, check_vma=False)
```

profile of v0, /device:TPU:0, one launch (start us, length us, event | category | flops | bytes accessed | tf_op | source)
XLA Modules:
  0.0 354.2 jit_solution(12946120193367616058)
XLA Ops:
  0.0 2.5 constant_dynamic-update-slice_fusion.1
  2.5 2.3 constant_dynamic-update-slice_fusion
  4.8 6.0 %collective-permute-start.1 = (bf16[512,2048]{1,0:T(8,128)(2,1)}, bf16[512,2048]{1,0:T(8,128)(2,1)}, u32[]{:S(2)}, u32[]{:S(2)}) collective-permute-start(bf16[512,2048]{1,0:T(8,128)(2,1)} %constant_dynamic-update-slice_fusion), channel_id=1, source_target_pairs={{4,0},{8,4},{12,8},{16,12},{20,16},{24,20},{28,24},{0,28},{5,1},{9... | collective-permute-start | bytes 6291464 | tf_op jit(solution)/shard_map/ppermute | solution.py:22
  10.8 0.0 collective-permute-start
  10.8 0.7 compare_select_fusion
  11.5 0.1 reshape.71
  11.6 0.7 broadcast_compare_fusion
  12.3 0.1 broadcast_bitcast_fusion
  12.3 4.0 %reshape.79 = bf16[4,128,16,64]{3,2,1,0:T(8,128)(2,1)} reshape(bf16[512,1024]{1,0:T(8,128)(2,1)} %param.14) | data formatting | bytes 2097152 | tf_op jit(solution)/shard_map/reshape | solution.py:59
  16.4 82.2 %collective-permute-done.1 = bf16[512,2048]{1,0:T(8,128)(2,1)} collective-permute-done((bf16[512,2048]{1,0:T(8,128)(2,1)}, bf16[512,2048]{1,0:T(8,128)(2,1)}, u32[]{:S(2)}, u32[]{:S(2)}) %collective-permute-start.1) | collective-permute-done | bytes 2097184 | tf_op jit(solution)/shard_map/ppermute | solution.py:22
  98.6 0.2 collective-permute-done
  98.8 5.9 %pad_maximum_fusion = bf16[1536,2048]{1,0:T(8,128)(2,1)} fusion(bf16[512,2048]{1,0:T(8,128)(2,1)} %collective-permute-done.1, bf16[512,2048]{1,0:T(8,128)(2,1)} %constant_dynamic-update-slice_fusion, bf16[512,2048]{1,0:T(8,128)(2,1)} %collective-permute-done), kind=kLoop, calls=%fused_computation.28 | loop fusion | flops 18874368 | bytes 12582912 | tf_op jit(solution)/shard_map/concatenate | solution.py:23
  104.7 10.1 %gather_fusion = bf16[32,128,2048]{2,1,0:T(8,128)(2,1)} fusion(bf16[12,128,2048]{2,1,0:T(8,128)(2,1)} %bitcast.64, s32[1024]{0:T(1024)S(1)} %pad_clamp_fusion), kind=kCustom, calls=%fused_computation | custom fusion | bytes 33554560 | tf_op jit(solution)/shard_map/gather | solution.py:56
  114.7 11.9 %fusion.66 = (bf16[4,8,128,1024]{3,2,1,0:T(8,128)(2,1)}, bf16[4,8,128,1024]{3,2,1,0:T(8,128)(2,1)}) fusion(bf16[4,8,128,2048]{3,2,1,0:T(8,128)(2,1)} %bitcast.65), kind=kLoop, calls=%fused_computation.88 | loop fusion | bytes 33554432 | tf_op jit(solution)/shard_map/slice | solution.py:57
  126.6 12.3 %copy.22 = bf16[4,8,128,1024]{2,1,3,0:T(8,128)(2,1)} copy(bf16[4,8,128,1024]{3,2,1,0:T(8,128)(2,1)} %get-tuple-element.6) | data formatting | bytes 16777216 | tf_op jit(solution)/shard_map/slice | solution.py:58
  138.9 13.3 %reshape.62 = bf16[4,1024,16,64]{1,3,2,0:T(8,128)(2,1)} reshape(bf16[4,8,128,1024]{2,1,3,0:T(8,128)(2,1)} %copy.22) | data formatting | bytes 16777216 | tf_op jit(solution)/shard_map/reshape | solution.py:58
  152.2 12.3 %copy.23 = bf16[4,8,128,1024]{2,1,3,0:T(8,128)(2,1)} copy(bf16[4,8,128,1024]{3,2,1,0:T(8,128)(2,1)} %get-tuple-element.5) | data formatting | bytes 16777216 | tf_op jit(solution)/shard_map/slice | solution.py:57
  164.6 13.3 %reshape.63 = bf16[4,1024,16,64]{1,3,2,0:T(8,128)(2,1)} reshape(bf16[4,8,128,1024]{2,1,3,0:T(8,128)(2,1)} %copy.23) | data formatting | bytes 16777216 | tf_op jit(solution)/shard_map/reshape | solution.py:57
  177.8 18.8 %fusion.67 = (f32[4,16,128]{2,1,0:T(8,128)S(1)}, f32[4,16,128,1024]{2,3,1,0:T(8,128)}) fusion(pred[4,1024]{1,0:T(4,128)(4,1)S(1)} %bitcast.69, bf16[4,1024,16,64]{1,3,2,0:T(8,128)(2,1)} %reshape.63, bf16[4,128,16,64]{3,2,1,0:T(8,128)(2,1)} %reshape.79), kind=kOutput, calls=%fused_computation.89 | convolution fusion | flops 1107297280 | bytes 43028480 | tf_op jit(solution)/shard_map/sub | solution.py:67
  196.6 14.6 %fusion.47 = bf16[4,128,16,64]{1,3,2,0:T(8,128)(2,1)S(1)} fusion(bf16[4,1024,16,64]{1,3,2,0:T(8,128)(2,1)} %reshape.62, f32[4,16,128,1024]{2,3,1,0:T(8,128)} %get-tuple-element.8, f32[4,16,128]{2,1,0:T(8,128)S(1)} %get-tuple-element.7), kind=kOutput, calls=%fused_computation.43 | convolution fusion | flops 1091043328 | bytes 43024384 | tf_op jit(solution)/shard_map/thqk,tkhd->tqhd/dot_general | solution.py:69
  211.3 0.0 copy-start.6
  211.3 0.9 copy.27
  212.2 2.6 multiply_reduce_fusion
  214.8 1.3 copy-done.2
  216.1 1.4 fusion.38
  217.5 54.7 %all_to_all.8 = bf16[32,1,32,1024]{3,2,1,0:T(8,128)(2,1)S(1)} all-to-all(bf16[32,1,32,1024]{3,2,1,0:T(8,128)(2,1)S(1)} %bitcast.68), channel_id=1, replica_groups=mesh['node'=8,'expert'=4] {'node','expert'}, dimensions={0} | all-to-all | bytes 4194304 | tf_op jit(solution)/shard_map/all_to_all | solution.py:87
  272.2 25.0 %fusion.29 = bf16[1024,1024]{1,0:T(8,128)(2,1)} fusion(bf16[1,4096,1024]{2,1,0:T(8,128)(2,1)} %param.25, bf16[1024,1024]{1,0:T(8,128)(2,1)S(1)} %bitcast.67, bf16[1,1024,4096]{2,1,0:T(8,128)(2,1)} %param.24), kind=kOutput, calls=%fused_computation.37 | convolution fusion | flops 17218666496 | bytes 20971520 | tf_op jit(solution)/shard_map/dot_general | solution.py:97
  297.2 3.8 %all-to-all-start.1 = ((bf16[1,32,32,1024]{3,2,0,1:T(8,128)(2,1)}), bf16[1,32,32,1024]{3,2,0,1:T(8,128)(2,1)}, u32[]{:S(2)}, u32[]{:S(2)}) async-start(bf16[1,32,32,1024]{3,2,0,1:T(8,128)(2,1)} %bitcast.10), calls=%async_computation.1 | async-start | bytes 4194304 | tf_op jit(solution)/shard_map/all_to_all | solution.py:98
  301.0 0.0 copy-start.1
  301.0 2.2 fusion.48
  303.3 46.4 %all-to-all-done.1 = bf16[1,32,32,1024]{3,2,0,1:T(8,128)(2,1)} async-done(((bf16[1,32,32,1024]{3,2,0,1:T(8,128)(2,1)}), bf16[1,32,32,1024]{3,2,0,1:T(8,128)(2,1)}, u32[]{:S(2)}, u32[]{:S(2)}) %all-to-all-start.1) | async-done | bytes 2097184 | tf_op jit(solution)/shard_map/all_to_all | solution.py:98
  349.7 4.5 %add_convert_fusion = bf16[512,1024]{1,0:T(8,128)(2,1)} fusion(f32[512,1024]{1,0:T(8,128)} %copy-done.2, bf16[1024,1024]{1,0:T(8,128)(2,1)} %bitcast.11, s32[512]{0:T(512)S(1)} %multiply_add_fusion, f32[512]{0:T(512)S(1)} %add_divide_fusion), kind=kOutput, calls=%fused_computation.30 | convolution fusion | flops 1075838976 | bytes 5246976 | tf_op jit(solution)/shard_map/ct,cd->td/dot_general | solution.py:102
  (18 shorter events, 0.1 us)
Async XLA Ops:
  0.0 212.2 %copy-start = (bf16[1024,1024]{1,0:T(8,128)(2,1)S(1)}, bf16[1024,1024]{1,0:T(8,128)(2,1)}, u32[]{:S(2)}) copy-start(bf16[1024,1024]{1,0:T(8,128)(2,1)} %param.19) | copy-start | bytes 6291460
  0.0 16.4 %copy-start.7 = (s32[512]{0:T(512)S(1)}, s32[512]{0:T(512)}, u32[]{:S(2)}) copy-start(s32[512]{0:T(512)} %param.23) | copy-start | bytes 6148
  0.0 16.4 %copy-start.4 = (s32[512]{0:T(512)S(1)}, s32[512]{0:T(512)}, u32[]{:S(2)}) copy-start(s32[512]{0:T(512)} %param.22) | copy-start | bytes 6148
  4.8 93.9 %collective-permute-start.1 = (bf16[512,2048]{1,0:T(8,128)(2,1)}, bf16[512,2048]{1,0:T(8,128)(2,1)}, u32[]{:S(2)}, u32[]{:S(2)}) collective-permute-start(bf16[512,2048]{1,0:T(8,128)(2,1)} %constant_dynamic-update-slice_fusion), channel_id=1, source_target_pairs={{4,0},{8,4},{12,8},{16,12},{20,16},{24,20},{28,24},{0,28},{5,1},{9... | collective-permute-start | bytes 6291464 | tf_op jit(solution)/shard_map/ppermute | solution.py:22
  10.8 88.0 %collective-permute-start = (bf16[512,2048]{1,0:T(8,128)(2,1)}, bf16[512,2048]{1,0:T(8,128)(2,1)}, u32[]{:S(2)}, u32[]{:S(2)}) collective-permute-start(bf16[512,2048]{1,0:T(8,128)(2,1)} %constant_dynamic-update-slice_fusion), channel_id=1, source_target_pairs={{0,4},{4,8},{8,12},{12,16},{16,20},{20,24},{24,28},{28,0},{1,5},{5... | collective-permute-start | bytes 6291464 | tf_op jit(solution)/shard_map/ppermute | solution.py:21
  211.3 4.9 %copy-start.6 = (f32[1024]{0:T(1024)S(1)}, f32[1024]{0:T(1024)}, u32[]{:S(2)}) copy-start(f32[1024]{0:T(1024)} %param.20) | copy-start | bytes 12292
  214.8 1.3 copy-start.2
  272.2 28.8 %copy-start.3 = (bf16[1024,32]{0,1:T(8,128)(2,1)S(1)}, bf16[1024,32]{0,1:T(8,128)(2,1)}, u32[]{:S(2)}) copy-start(bf16[1024,32]{0,1:T(8,128)(2,1)} %param.21) | copy-start | bytes 196612
  272.2 28.8 %copy-start.5 = (s32[512]{0:T(512)S(1)}, s32[512]{0:T(512)}, u32[]{:S(2)}) copy-start(s32[512]{0:T(512)} %param.22) | copy-start | bytes 6148
  297.2 52.5 %all-to-all-start.1 = ((bf16[1,32,32,1024]{3,2,0,1:T(8,128)(2,1)}), bf16[1,32,32,1024]{3,2,0,1:T(8,128)(2,1)}, u32[]{:S(2)}, u32[]{:S(2)}) async-start(bf16[1,32,32,1024]{3,2,0,1:T(8,128)(2,1)} %bitcast.10), calls=%async_computation.1 | async-start | bytes 4194304 | tf_op jit(solution)/shard_map/all_to_all | solution.py:98
  301.0 53.2 %copy-start.1 = (bf16[1024,1024]{1,0:T(8,128)(2,1)S(1)}, bf16[1024,1024]{1,0:T(8,128)(2,1)}, u32[]{:S(2)}) copy-start(bf16[1024,1024]{1,0:T(8,128)(2,1)} %param.19) | copy-start | bytes 6291460
where the time goes:
time: 356 us; the launch traced here: 354 us
  waiting for transfers between devices  129 us (36%)
  local copies, waits for them, and re-layouts  84.3 us (24%)
  matrix products  69.1 us (19%)
  blocking collectives  54.7 us (15%)
  starting transfers between devices  9.8 us (3%)
  other arithmetic  7.34 us (2%)
    ppermute x1, waiting for transfers between devices, extended(): after = lax.ppermute(leading, axis, down)  82.2 us
    all_to_all x1, blocking collectives, shards(): lax.all_to_all(outgoing.reshape(experts, 1, cap, D), ('node', 'expert'),...  54.7 us
    all_to_all x1, waiting for transfers between devices, shards(): lax.all_to_all(result.reshape(block.shape), ('node', 'expert'), split_axi...  46.4 us
    dot_general x1, matrix products, shards(): jnp.dot(lifted, down_matrix, preferred_element_type=jnp.float32)  25 us
    slice x2, local copies, waits for them, and re-layouts, shards(): near_keys = gathered[..., :D].reshape(tiles_dev, NB * TILE, HEADS, HEAD_DIM)  24.2 us
    sub x1, matrix products, shards(): weights = jnp.exp(masked - peak)  18.8 us
    dot_general x1, matrix products, shards(): jnp.einsum('thqk,tkhd->tqhd', weights, near_values, preferred_element_typ...  14.6 us
    reshape x1, local copies, waits for them, and re-layouts, shards(): gathered[..., D:].reshape(tiles_dev, NB * TILE, HEADS, HEAD_DIM)  13.3 us
  transfers between devices with their start and end apart: 3, of which 3 were waited for; matrix products, arithmetic and copies ran while one was open for 2% of the time, Pallas kernels for 0%

commit v1 on v0

--- a/solution.py
+++ b/solution.py
@@ -84,12 +84,18 @@
     outgoing = jnp.dot(one_hot, normed, preferred_element_type=jnp.float32).astype(jnp.bfloat16)
     up_matrix = w_up[0]
     down_matrix = w_down[0]
-    block = lax.all_to_all(
-        outgoing.reshape(experts, 1, cap, D),
-        ("node", "expert"),
-        split_axis=0,
-        concat_axis=1,
-        tiled=True,
+    block = jnp.concatenate(
+        lax.all_to_all(
+            jnp.stack(
+                jnp.split(
+                    outgoing.reshape(experts, 1, cap, D), lax.axis_size(("node", "expert")), axis=0
+                )
+            ),
+            ("node", "expert"),
+            0,
+            0,
+        ),
+        axis=1,
     )
     token_rows = block.reshape(-1, D)
     lifted = jnp.dot(token_rows, up_matrix, preferred_element_type=jnp.float32)

time: 356 us -> 354 us (level)
  waiting for transfers between devices: 129 us -> 134 us
  local copies, waits for them, and re-layouts: 84.3 us -> 80.7 us
  transfers between devices with their start and end apart: 3 -> 3, of which waited for: 3 -> 3; matrix products, arithmetic and copies ran while one was open for 2% -> 1% of each run, Pallas kernels for 0% -> 0%
where the time goes in v1:
time: 354 us; the launch traced here: 352 us
  waiting for transfers between devices  134 us (38%)
  local copies, waits for them, and re-layouts  80.7 us (23%)
  matrix products  66.9 us (19%)
  blocking collectives  54.8 us (15%)
  starting transfers between devices  9.8 us (3%)
  other arithmetic  5.97 us (2%)
    ppermute x1, waiting for transfers between devices, extended(): after = lax.ppermute(leading, axis, down)  85.2 us
    all_to_all x1, blocking collectives, shards(): lax.all_to_all(jnp.stack(jnp.split(outgoing.reshape(experts, 1, cap, D),...  54.8 us
    all_to_all x1, waiting for transfers between devices, shards(): lax.all_to_all(result.reshape(block.shape), ('node', 'expert'), split_axi...  48.1 us
    dot_general x1, matrix products, shards(): jnp.dot(lifted, down_matrix, preferred_element_type=jnp.float32)  25.5 us
    slice x2, local copies, waits for them, and re-layouts, shards(): near_keys = gathered[..., :D].reshape(tiles_dev, NB * TILE, HEADS, HEAD_DIM)  24.2 us
    sub x1, matrix products, shards(): weights = jnp.exp(masked - peak)  18.8 us
    dot_general x1, matrix products, shards(): jnp.einsum('thqk,tkhd->tqhd', weights, near_values, preferred_element_typ...  14.6 us
    reshape x1, local copies, waits for them, and re-layouts, shards(): gathered[..., D:].reshape(tiles_dev, NB * TILE, HEADS, HEAD_DIM)  13.3 us
  transfers between devices with their start and end apart: 3, of which 3 were waited for; matrix products, arithmetic and copies ran while one was open for 1% of the time, Pallas kernels for 0%

profile of v1, /device:TPU:0, one launch (start us, length us, event | category | flops | bytes accessed | tf_op | source)
XLA Modules:
  0.0 352.1 jit_solution(10449588060041755676)
XLA Ops:
  0.0 0.0 copy-start
  0.0 0.0 copy-start.4
  0.0 2.5 constant_dynamic-update-slice_fusion.1
  2.5 1.1 constant_dynamic-update-slice_fusion
  3.6 6.0 %collective-permute-start.1 = (bf16[512,2048]{1,0:T(8,128)(2,1)}, bf16[512,2048]{1,0:T(8,128)(2,1)}, u32[]{:S(2)}, u32[]{:S(2)}) collective-permute-start(bf16[512,2048]{1,0:T(8,128)(2,1)} %constant_dynamic-update-slice_fusion), channel_id=1, source_target_pairs={{4,0},{8,4},{12,8},{16,12},{20,16},{24,20},{28,24},{0,28},{5,1},{9... | collective-permute-start | bytes 6291464 | tf_op jit(solution)/shard_map/ppermute | solution.py:22
  9.6 0.0 collective-permute-start
  9.6 0.1 reshape.124
  9.7 0.1 broadcast_bitcast_fusion
  9.8 2.4 reshape.132
  12.2 0.0 copy-done.8
  12.2 85.2 %collective-permute-done.1 = bf16[512,2048]{1,0:T(8,128)(2,1)} collective-permute-done((bf16[512,2048]{1,0:T(8,128)(2,1)}, bf16[512,2048]{1,0:T(8,128)(2,1)}, u32[]{:S(2)}, u32[]{:S(2)}) %collective-permute-start.1) | collective-permute-done | bytes 2097184 | tf_op jit(solution)/shard_map/ppermute | solution.py:22
  97.4 0.2 collective-permute-done
  97.6 5.9 %pad_maximum_fusion = bf16[1536,2048]{1,0:T(8,128)(2,1)} fusion(bf16[512,2048]{1,0:T(8,128)(2,1)} %collective-permute-done.1, bf16[512,2048]{1,0:T(8,128)(2,1)} %constant_dynamic-update-slice_fusion, bf16[512,2048]{1,0:T(8,128)(2,1)} %collective-permute-done), kind=kLoop, calls=%fused_computation.28 | loop fusion | flops 18874368 | bytes 12582912 | tf_op jit(solution)/shard_map/concatenate | solution.py:23
  103.5 10.1 %gather_fusion = bf16[32,128,2048]{2,1,0:T(8,128)(2,1)} fusion(bf16[12,128,2048]{2,1,0:T(8,128)(2,1)} %bitcast.189, s32[1024]{0:T(1024)S(1)} %pad_clamp_fusion), kind=kCustom, calls=%fused_computation | custom fusion | bytes 33554560 | tf_op jit(solution)/shard_map/gather | solution.py:56
  113.6 11.9 %fusion.66 = (bf16[4,8,128,1024]{3,2,1,0:T(8,128)(2,1)}, bf16[4,8,128,1024]{3,2,1,0:T(8,128)(2,1)}) fusion(bf16[4,8,128,2048]{3,2,1,0:T(8,128)(2,1)} %bitcast.190), kind=kLoop, calls=%fused_computation.152 | loop fusion | bytes 33554432 | tf_op jit(solution)/shard_map/slice | solution.py:57
  125.4 12.3 %copy.22 = bf16[4,8,128,1024]{2,1,3,0:T(8,128)(2,1)} copy(bf16[4,8,128,1024]{3,2,1,0:T(8,128)(2,1)} %get-tuple-element.6) | data formatting | bytes 16777216 | tf_op jit(solution)/shard_map/slice | solution.py:58
  137.7 13.3 %reshape.117 = bf16[4,1024,16,64]{1,3,2,0:T(8,128)(2,1)} reshape(bf16[4,8,128,1024]{2,1,3,0:T(8,128)(2,1)} %copy.22) | data formatting | bytes 16777216 | tf_op jit(solution)/shard_map/reshape | solution.py:58
  151.1 12.3 %copy.23 = bf16[4,8,128,1024]{2,1,3,0:T(8,128)(2,1)} copy(bf16[4,8,128,1024]{3,2,1,0:T(8,128)(2,1)} %get-tuple-element.5) | data formatting | bytes 16777216 | tf_op jit(solution)/shard_map/slice | solution.py:57
  163.4 13.3 %reshape.118 = bf16[4,1024,16,64]{1,3,2,0:T(8,128)(2,1)} reshape(bf16[4,8,128,1024]{2,1,3,0:T(8,128)(2,1)} %copy.23) | data formatting | bytes 16777216 | tf_op jit(solution)/shard_map/reshape | solution.py:57
  176.7 18.8 %fusion.67 = (f32[4,16,128]{2,1,0:T(8,128)S(1)}, f32[4,16,128,1024]{2,3,1,0:T(8,128)}) fusion(pred[4,1024]{1,0:T(4,128)(4,1)S(1)} %bitcast.194, bf16[4,1024,16,64]{1,3,2,0:T(8,128)(2,1)} %reshape.118, bf16[4,128,16,64]{3,2,1,0:T(8,128)(2,1)} %reshape.132), kind=kOutput, calls=%fused_computation.153 | convolution fusion | flops 1107297280 | bytes 43028480 | tf_op jit(solution)/shard_map/sub | solution.py:67
  195.5 14.6 %fusion.47 = bf16[4,128,16,64]{1,3,2,0:T(8,128)(2,1)S(1)} fusion(bf16[4,1024,16,64]{1,3,2,0:T(8,128)(2,1)} %reshape.117, f32[4,16,128,1024]{2,3,1,0:T(8,128)} %get-tuple-element.8, f32[4,16,128]{2,1,0:T(8,128)S(1)} %get-tuple-element.7), kind=kOutput, calls=%fused_computation.43 | convolution fusion | flops 1091043328 | bytes 43024384 | tf_op jit(solution)/shard_map/thqk,tkhd->tqhd/dot_general | solution.py:69
  210.2 0.0 copy-start.6
  210.2 0.9 copy.27
  211.1 0.3 copy-done.6
  211.4 1.4 multiply_reduce_fusion
  212.8 1.4 fusion.38
  214.7 54.8 %all_to_all.14 = bf16[32,1,1,32,1024]{4,3,2,1,0:T(8,128)(2,1)} all-to-all(bf16[32,1,1,32,1024]{4,3,2,1,0:T(8,128)(2,1)S(1)} %constant_dynamic-update-slice_fusion.2), channel_id=1, replica_groups=mesh['node'=8,'expert'=4] {'node','expert'}, dimensions={0} | all-to-all | bytes 4194304 | tf_op jit(solution)/shard_map/all_to_all | solution.py:88
  269.4 25.5 %fusion.29 = bf16[1024,1024]{1,0:T(8,128)(2,1)} fusion(bf16[1,4096,1024]{2,1,0:T(8,128)(2,1)} %param.25, bf16[1024,1024]{1,0:T(8,128)(2,1)} %bitcast.193, bf16[1,1024,4096]{2,1,0:T(8,128)(2,1)} %param.24), kind=kOutput, calls=%fused_computation.37 | convolution fusion | flops 17218666496 | bytes 20971520 | tf_op jit(solution)/shard_map/dot_general | solution.py:103
  295.0 3.8 %all-to-all-start.1 = ((bf16[1,32,32,1024]{3,2,0,1:T(8,128)(2,1)}), bf16[1,32,32,1024]{3,2,0,1:T(8,128)(2,1)}, u32[]{:S(2)}, u32[]{:S(2)}) async-start(bf16[1,32,32,1024]{3,2,0,1:T(8,128)(2,1)} %bitcast.192), calls=%async_computation.1 | async-start | bytes 4194304 | tf_op jit(solution)/shard_map/all_to_all | solution.py:104
  298.8 0.5 fusion.48
  299.3 48.1 %all-to-all-done.1 = bf16[1,32,32,1024]{3,2,0,1:T(8,128)(2,1)} async-done(((bf16[1,32,32,1024]{3,2,0,1:T(8,128)(2,1)}), bf16[1,32,32,1024]{3,2,0,1:T(8,128)(2,1)}, u32[]{:S(2)}, u32[]{:S(2)}) %all-to-all-start.1) | async-done | bytes 2097184 | tf_op jit(solution)/shard_map/all_to_all | solution.py:104
  347.5 4.6 %add_convert_fusion = bf16[512,1024]{1,0:T(8,128)(2,1)} fusion(f32[512,1024]{1,0:T(8,128)} %copy-done.2, bf16[1024,1024]{1,0:T(8,128)(2,1)} %bitcast.41, s32[512]{0:T(512)S(1)} %multiply_add_fusion, f32[512]{0:T(512)S(1)} %add_divide_fusion), kind=kOutput, calls=%fused_computation.30 | convolution fusion | flops 1075838976 | bytes 5246976 | tf_op jit(solution)/shard_map/ct,cd->td/dot_general | solution.py:108
  (62 shorter events, 0.3 us)
Async XLA Ops:
  0.0 211.1 %copy-start = (bf16[1024,1024]{1,0:T(8,128)(2,1)S(1)}, bf16[1024,1024]{1,0:T(8,128)(2,1)}, u32[]{:S(2)}) copy-start(bf16[1024,1024]{1,0:T(8,128)(2,1)} %param.19) | copy-start | bytes 6291460
  0.0 2.5 copy-start.5
  0.0 9.6 %copy-start.13 = (s32[4,8]{1,0:T(4,128)S(1)}, s32[4,8]{1,0:T(4,128)}, u32[]{:S(2)}) copy-start(s32[4,8]{1,0:T(4,128)} %param.17) | copy-start | bytes 388
  0.0 9.7 %copy-start.12 = (s32[4,8]{1,0:T(4,128)S(1)}, s32[4,8]{1,0:T(4,128)}, u32[]{:S(2)}) copy-start(s32[4,8]{1,0:T(4,128)} %param.18) | copy-start | bytes 388
  0.0 9.8 %copy-start.4 = (bf16[512,1024]{1,0:T(8,128)(2,1)S(1)}, bf16[512,1024]{1,0:T(8,128)(2,1)}, u32[]{:S(2)}) copy-start(bf16[512,1024]{1,0:T(8,128)(2,1)} %param.14) | copy-start | bytes 3145732
  3.6 8.6 %copy-start.8 = (s32[512]{0:T(512)S(1)}, s32[512]{0:T(512)}, u32[]{:S(2)}) copy-start(s32[512]{0:T(512)} %param.22) | copy-start | bytes 6148
  3.6 8.6 %copy-start.11 = (s32[512]{0:T(512)S(1)}, s32[512]{0:T(512)}, u32[]{:S(2)}) copy-start(s32[512]{0:T(512)} %param.23) | copy-start | bytes 6148
  3.6 93.9 %collective-permute-start.1 = (bf16[512,2048]{1,0:T(8,128)(2,1)}, bf16[512,2048]{1,0:T(8,128)(2,1)}, u32[]{:S(2)}, u32[]{:S(2)}) collective-permute-start(bf16[512,2048]{1,0:T(8,128)(2,1)} %constant_dynamic-update-slice_fusion), channel_id=1, source_target_pairs={{4,0},{8,4},{12,8},{16,12},{20,16},{24,20},{28,24},{0,28},{5,1},{9... | collective-permute-start | bytes 6291464 | tf_op jit(solution)/shard_map/ppermute | solution.py:22
  9.6 88.0 %collective-permute-start = (bf16[512,2048]{1,0:T(8,128)(2,1)}, bf16[512,2048]{1,0:T(8,128)(2,1)}, u32[]{:S(2)}, u32[]{:S(2)}) collective-permute-start(bf16[512,2048]{1,0:T(8,128)(2,1)} %constant_dynamic-update-slice_fusion), channel_id=1, source_target_pairs={{0,4},{4,8},{8,12},{12,16},{16,20},{20,24},{24,28},{28,0},{1,5},{5... | collective-permute-start | bytes 6291464 | tf_op jit(solution)/shard_map/ppermute | solution.py:21
  210.2 1.2 copy-start.6
  211.4 1.4 copy-start.10
  212.8 1.4 copy-start.2
  295.0 3.8 %copy-start.3 = (f32[512,1024]{1,0:T(8,128)S(1)}, f32[512,1024]{1,0:T(8,128)}, u32[]{:S(2)}) copy-start(f32[512,1024]{1,0:T(8,128)} %copy-done.2) | copy-start | bytes 6291460
  295.0 3.8 %copy-start.7 = (bf16[1024,32]{0,1:T(8,128)(2,1)S(1)}, bf16[1024,32]{0,1:T(8,128)(2,1)}, u32[]{:S(2)}) copy-start(bf16[1024,32]{0,1:T(8,128)(2,1)} %param.21) | copy-start | bytes 196612
  295.0 3.8 %copy-start.9 = (s32[512]{0:T(512)S(1)}, s32[512]{0:T(512)}, u32[]{:S(2)}) copy-start(s32[512]{0:T(512)} %param.22) | copy-start | bytes 6148
  295.0 52.5 %all-to-all-start.1 = ((bf16[1,32,32,1024]{3,2,0,1:T(8,128)(2,1)}), bf16[1,32,32,1024]{3,2,0,1:T(8,128)(2,1)}, u32[]{:S(2)}, u32[]{:S(2)}) async-start(bf16[1,32,32,1024]{3,2,0,1:T(8,128)(2,1)} %bitcast.192), calls=%async_computation.1 | async-start | bytes 4194304 | tf_op jit(solution)/shard_map/all_to_all | solution.py:104
  347.5 4.6 %copy-start.1 = (bf16[1024,1024]{1,0:T(8,128)(2,1)S(1)}, bf16[1024,1024]{1,0:T(8,128)(2,1)}, u32[]{:S(2)}) copy-start(bf16[1024,1024]{1,0:T(8,128)(2,1)} %param.19) | copy-start | bytes 6291460
